TPU v7x, 32 devices: a whole 2x2x4 slice. The times are simulated.
32 devices in a mesh: hap: 16 (over z, x, core), mk: 2 (over y).
Axes of the slice: x: 2, y: 2, z: 4, core: 2. Of those that a mesh axis runs over, the one named last changes fastest.
Arguments:
- posterior: bfloat16 [10, 1024, 16384], P('mk', None, 'hap'), may hold values from 0 to 1, as said below
- alleles: int32 [16384, 64], P('hap', 'mk'), may hold values from 0 to 1
- owner_map: int32 [1024], replicated, may hold values from 0 to 31, as said below
Outputs:
- dosage: float32 [1024, 64], P(('hap', 'mk'))
Inputs may be any that keep to these rules, and one draw needn't show every extreme that they name: `owner_map`: every device index is named by exactly 32 targets. `posterior`: every entry is positive.
All inputs are finite; a program needn't handle non-finite values.
Results may differ from a plain program's by a relative error of at most 0.0003.
Values sent between devices are 32-bit elements; how exact they have to be, the bound alone decides.
A program may use at most 64 MiB of HBM per device.

v0:
```python
import functools

import jax
import jax.numpy as jnp
from jax import lax
from jax.experimental import pallas as pl
from jax.experimental.pallas import tpu as pltpu
from jax.sharding import PartitionSpec as P

LANES = 128
HALF = LANES // 2
CORES = 2
MESH = pl.DeviceIdType.MESH
F32 = jnp.float32
BF16 = jnp.bfloat16


def own_rows(ref, index, count):
    if count % 8 == 0:
        return ref[pl.ds(pl.multiple_of(index * count, 8), count), :]
    pieces = 8 // count
    tile = ref[pl.ds(pl.multiple_of((index // pieces) * 8, 8), 8), :]
    rows = tile[:count]
    for piece in range(1, pieces):
        rows = jnp.where(index % pieces == piece, tile[piece * count : (piece + 1) * count], rows)
    return rows


def kernel(
    hap_count,
    mk_count,
    steps,
    post_hbm,
    allele_hbm,
    owner_hbm,
    out_ref,
    post,
    allele,
    owner,
    weights,
    choose,
    parts,
    mine,
    pair_in,
    reduced,
    chip_in,
    final,
    turned,
    post_sem,
    small_sem,
    pair_send,
    pair_recv,
    chip_send,
    chip_recv,
    final_send,
    final_recv,
):
    anchors, targets, _ = post.shape
    block = allele.shape[0]
    intervals = anchors - 1
    span = block // intervals
    local = intervals // CORES
    body = 2 * local * span
    rows_kept = mine.shape[1] // CORES
    chips = hap_count // CORES
    per_chip = targets // chips
    devices = hap_count * mk_count
    per_device = targets // devices
    group = CORES * mk_count
    chunk = targets // steps

    hap, mk = lax.axis_index("hap"), lax.axis_index("mk")
    chip, core = hap // CORES, hap % CORES
    place = mk * CORES + core

    def chip_peer(step):
        return {"hap": ((chip + step) % chips) * CORES + core, "mk": mk}

    def group_peer(step):
        other = (place + step) % group
        return {"hap": chip * CORES + other % CORES, "mk": other // CORES}

    allele_copy = pltpu.make_async_copy(allele_hbm, allele, small_sem.at[0])
    owner_copy = pltpu.make_async_copy(owner_hbm, owner, small_sem.at[1])
    allele_copy.start()
    post_copies = []
    for i in range(steps):
        rows = pl.ds(i * chunk, chunk)
        copy = pltpu.make_async_copy(post_hbm.at[:, rows, :], post.at[:, rows, :], post_sem.at[i])
        copy.start()
        post_copies.append(copy)
        if i == 0:
            owner_copy.start()

    barrier = pltpu.get_barrier_semaphore()
    for step in range(1, chips):
        pl.semaphore_signal(barrier, inc=1, device_id=chip_peer(step), device_id_type=MESH)
    for step in range(1, group):
        pl.semaphore_signal(barrier, inc=1, device_id=group_peer(step), device_id_type=MESH)

    order = sorted(range(1, chips), key=lambda s: abs(s - chips // 2 - 0.5)) + [0]

    allele_copy.wait()
    col = lax.broadcasted_iota(jnp.int32, (block, LANES), 1)
    marker = lax.broadcasted_iota(jnp.int32, (block, LANES), 0)
    lane = lax.broadcasted_iota(jnp.int32, (1, LANES), 1)
    spread = jnp.zeros((block, LANES), F32)
    starts = []
    for j in range(intervals):
        for side in range(2):
            start = (j // local) * HALF + (j % local) * 2 * span + side * span
            starts.append((j + side, start))
            hit = (col - start == marker - j * span) & (col >= start) & (col < start + span)
            spread = spread + hit.astype(F32)
    wide = lax.dot_general(
        allele[...].astype(F32).astype(BF16),
        spread.astype(BF16),
        (((0,), (0,)), ((), ())),
        preferred_element_type=F32,
    )
    for k in range(anchors):
        inside = jnp.zeros((1, LANES), F32)
        for anchor, start in starts:
            if anchor == k:
                inside = inside + ((lane >= start) & (lane < start + span)).astype(F32)
        ones = jnp.zeros((1, LANES), F32)
        for c in range(CORES):
            if c * local <= k <= (c + 1) * local:
                ones = ones + (lane == c * HALF + body + k - c * local).astype(F32)
        weights[k] = (wide * inside + ones).astype(BF16)

    for i in range(steps):
        rows = pl.ds(i * chunk, chunk)
        post_copies[i].wait()
        if i == 0:
            owner_copy.wait()
            owners = owner[...]
            table = (lax.broadcasted_iota(jnp.int32, (devices, targets), 0) == owners).astype(F32)
            before = (
                lax.broadcasted_iota(jnp.int32, (LANES, LANES), 0)
                < lax.broadcasted_iota(jnp.int32, (LANES, LANES), 1)
            ).astype(F32).astype(BF16)
            carry = jnp.zeros((devices, 1), F32)
            ranks = []
            for b in range(targets // LANES):
                piece = table[:, b * LANES : (b + 1) * LANES]
                count = jnp.dot(piece.astype(BF16), before, preferred_element_type=F32) + carry
                ranks.append(jnp.sum(piece * count, axis=0, keepdims=True))
                carry = carry + jnp.sum(piece, axis=1, keepdims=True)
            row_of = owners.astype(F32) * per_device + jnp.concatenate(ranks, axis=1)
        for step in order[i::steps]:
            first = ((chip + step) % chips) * per_chip
            wanted = (lax.broadcasted_iota(jnp.int32, (per_chip, targets), 0) + first).astype(F32)
            choose[step] = (wanted == row_of).astype(F32).astype(BF16)
        total = jnp.dot(post[0, rows, :], weights[0], preferred_element_type=F32)
        for k in range(1, anchors):
            total = total + jnp.dot(post[k, rows, :], weights[k], preferred_element_type=F32)
        high = total.astype(BF16)
        parts[rows, pl.ds(0, LANES)] = high
        parts[rows, pl.ds(LANES, LANES)] = (total - high.astype(F32)).astype(BF16)

    pl.semaphore_wait(barrier, chips - 1 + group - 1)

    kept = pl.ds(pl.multiple_of(core * rows_kept, 8), rows_kept)
    given = pl.ds(pl.multiple_of((1 - core) * rows_kept, 8), rows_kept)
    pair_copies = {}
    chip_copies = {}
    lag = 3

    def pass_on(step):
        pair_copies[step].wait_recv()
        reduced[step] = mine[step, kept, :] + pair_in[step]
        if step:
            copy = pltpu.make_async_remote_copy(
                src_ref=reduced.at[step],
                dst_ref=chip_in.at[step],
                send_sem=chip_send.at[step],
                recv_sem=chip_recv.at[step],
                device_id=chip_peer(step),
                device_id_type=MESH,
            )
            copy.start()
            chip_copies[step] = copy

    for at, step in enumerate(order):
        both = jnp.dot(choose[step], parts[...], preferred_element_type=F32)
        sums = jnp.transpose(both[:, :LANES] + both[:, LANES:])
        for c in range(CORES):
            mine[step, pl.ds(c * rows_kept, rows_kept), :] = sums[c * HALF : c * HALF + rows_kept]
        copy = pltpu.make_async_remote_copy(
            src_ref=mine.at[step, given],
            dst_ref=pair_in.at[step],
            send_sem=pair_send.at[step],
            recv_sem=pair_recv.at[step],
            device_id={"hap": chip * CORES + 1 - core, "mk": mk},
            device_id_type=MESH,
        )
        copy.start()
        pair_copies[step] = copy
        if at >= lag:
            pass_on(order[at - lag])

    for step in order[-lag:]:
        pass_on(step)

    total = reduced[0]
    for step in reversed(order[:-1]):
        chip_copies[step].wait_recv()
        total = total + chip_in[step]

    weight = (lax.broadcasted_iota(jnp.int32, (span, per_chip), 0).astype(F32) + 0.5) / span
    for l in range(local):
        base = 2 * l * span
        left = total[base : base + span] / total[body + l : body + l + 1]
        right = total[base + span : base + 2 * span] / total[body + l + 1 : body + l + 2]
        final[place, pl.ds(l * span, span), :] = (1.0 - weight) * left + weight * right

    final_copies = {}
    for step in range(1, group):
        copy = pltpu.make_async_remote_copy(
            src_ref=final.at[place],
            dst_ref=final.at[place],
            send_sem=final_send.at[step],
            recv_sem=final_recv.at[step],
            device_id=group_peer(step),
            device_id_type=MESH,
        )
        copy.start()
        final_copies[step] = copy
    for step in range(1, group):
        source = (place + group - step) % group
        pltpu.make_async_remote_copy(
            src_ref=final.at[source],
            dst_ref=final.at[source],
            send_sem=final_send.at[step],
            recv_sem=final_recv.at[step],
            device_id=group_peer(step),
            device_id_type=MESH,
        ).wait_recv()

    all_markers = final[...].reshape(group * local * span, per_chip)
    turned[...] = jnp.transpose(all_markers)
    out_ref[...] = own_rows(turned, core * mk_count + mk, per_device)

    for step in order:
        pair_copies[step].wait_send()
        if step:
            chip_copies[step].wait_send()
    for step in range(1, group):
        final_copies[step].wait_send()


def solution(mesh):
    hap_count, mk_count = mesh.shape["hap"], mesh.shape["mk"]
    steps = 4

    def on_device(posterior, alleles, owner_map):
        anchors, targets, refs = posterior.shape
        block = alleles.shape[1]
        intervals = anchors - 1
        local = intervals // CORES
        span = block // intervals
        chips = hap_count // CORES
        per_chip = targets // chips
        per_device = targets // (hap_count * mk_count)
        group = CORES * mk_count
        rows_kept = -(-(2 * local * span + local + 1) // 8) * 8
        scratch = [
            pltpu.VMEM(posterior.shape, BF16),
            pltpu.VMEM((block, refs), jnp.int32),
            pltpu.VMEM((1, targets), jnp.int32),
            pltpu.VMEM((anchors, refs, LANES), BF16),
            pltpu.VMEM((chips, per_chip, targets), BF16),
            pltpu.VMEM((targets, 2 * LANES), BF16),
            pltpu.VMEM((chips, CORES * rows_kept, per_chip), F32),
            pltpu.VMEM((chips, rows_kept, per_chip), F32),
            pltpu.VMEM((chips, rows_kept, per_chip), F32),
            pltpu.VMEM((chips, rows_kept, per_chip), F32),
            pltpu.VMEM((group, local * span, per_chip), F32),
            pltpu.VMEM((per_chip, mk_count * block), F32),
            pltpu.SemaphoreType.DMA((steps,)),
            pltpu.SemaphoreType.DMA((2,)),
        ] + [pltpu.SemaphoreType.DMA((chips,))] * 4 + [pltpu.SemaphoreType.DMA((group,))] * 2
        return pl.pallas_call(
            functools.partial(kernel, hap_count, mk_count, steps),
            out_shape=jax.ShapeDtypeStruct((per_device, mk_count * block), F32),
            in_specs=[pl.BlockSpec(memory_space=pltpu.HBM)] * 3,
            out_specs=pl.BlockSpec(memory_space=pltpu.VMEM),
            scratch_shapes=scratch,
            compiler_params=pltpu.CompilerParams(
                collective_id=0, has_side_effects=True, vmem_limit_bytes=48 * 1024 * 1024
            ),
        )(posterior, alleles.T, owner_map.reshape(1, targets))

    placed = (P("mk", None, "hap"), P("hap", "mk"), P())
    return jax.shard_map(
        on_device, mesh=mesh, in_specs=placed, out_specs=P(("hap", "mk"), None), check_vma=False
    )
```

profile of v0, /device:TPU:0, one launch (start us, length us, event | category | flops | bytes accessed | tf_op | source)
XLA Modules:
  0.0 22.5 jit_solution(6736243850752889847)
XLA Ops:
  0.0 0.0 copy-start
  0.0 0.9 %copy-done = s32[1024,32]{0,1:T(8,128)S(1)} copy-done((s32[1024,32]{0,1:T(8,128)S(1)}, s32[1024,32]{0,1:T(8,128)}, u32[]{:S(2)}) %copy-start) | copy-done | bytes 131096
  0.9 0.0 copy-start.1
  0.9 0.7 %copy-done.1 = s32[1024]{0:T(1024)S(1)} copy-done((s32[1024]{0:T(1024)S(1)}, s32[1024]{0:T(1024)}, u32[]{:S(2)}) %copy-start.1) | copy-done | bytes 4120
  1.6 20.3 %shard_map.37 = f32[32,64]{1,0:T(8,128)S(1)} custom-call(bf16[5,1024,1024]{2,1,0:T(8,128)(2,1)} %post_hbm.1, s32[32,1024]{1,0:T(8,128)S(1)} %bitcast.2, s32[1,1024]{1,0:T(1,128)S(1)} %bitcast.3), custom_call_target="tpu_custom_call" | custom-call | tf_op jit(solution)/shard_map/pallas_call | solution.py:284
  21.9 0.6 %copy.5 = f32[32,64]{1,0:T(8,128)} copy(f32[32,64]{1,0:T(8,128)S(1)} %shard_map.37) | data formatting | bytes 16384
Async XLA Ops:
  0.0 0.9 %copy-start = (s32[1024,32]{0,1:T(8,128)S(1)}, s32[1024,32]{0,1:T(8,128)}, u32[]{:S(2)}) copy-start(s32[1024,32]{0,1:T(8,128)} %param.4) | copy-start | bytes 393220
  0.9 0.7 %copy-start.1 = (s32[1024]{0:T(1024)S(1)}, s32[1024]{0:T(1024)}, u32[]{:S(2)}) copy-start(s32[1024]{0:T(1024)} %param.5) | copy-start | bytes 12292
where the time goes:
time: 22.6 us; the launch traced here: 22.5 us
  Pallas kernels  20.3 us (90%)
  local copies, waits for them, and re-layouts  2.2 us (10%)
    pallas_call x1, Pallas kernels, on_device(): pl.pallas_call(functools.partial(kernel, hap_count, mk_count, steps), out...  20.3 us
    unnamed x5, local copies, waits for them, and re-layouts  2.2 us

commit v1 on v0

v1 whole, which is shorter than its diff:
```python
import functools

import jax
import jax.numpy as jnp
from jax import lax
from jax.experimental import pallas as pl
from jax.experimental.pallas import tpu as pltpu
from jax.sharding import PartitionSpec as P

LANES = 128
CORES = 2
GROUPS = 2
SIDES = 2
MESH = pl.DeviceIdType.MESH
F32 = jnp.float32
BF16 = jnp.bfloat16


def block_transpose(tiles, width):
    lane = lax.broadcasted_iota(jnp.int32, tiles[0].shape, 1) // width
    count = len(tiles)
    bit = 1
    while bit < count:
        swapped = list(tiles)
        low = lane // bit % 2 == 0
        for i in range(count):
            if i & bit == 0:
                a, b = tiles[i], tiles[i + bit]
                swapped[i] = jnp.where(low, a, pltpu.roll(b, bit * width, 1))
                swapped[i + bit] = jnp.where(low, pltpu.roll(a, LANES - bit * width, 1), b)
        tiles = swapped
        bit *= 2
    return tiles


def kernel(
    hap_count,
    mk_count,
    steps,
    post_hbm,
    allele_hbm,
    owner_hbm,
    out_ref,
    post,
    allele,
    owner,
    weights,
    choose,
    held,
    parts,
    mine,
    pair_in,
    reduced,
    inbox,
    stack,
    post_sem,
    small_sem,
    pair_send,
    pair_recv,
    chip_send,
    chip_recv,
):
    anchors, targets, refs = post.shape
    block = allele.shape[0]
    intervals = anchors - 1
    span = block // intervals
    local = intervals // GROUPS
    blocks = local * SIDES
    width = LANES // blocks
    pitch = 2 * span
    half = blocks * pitch
    rows_sent = span + 1
    chips = hap_count // CORES
    devices = hap_count * mk_count
    per_device = targets // devices
    per_chip = CORES * mk_count
    tiles_per_chip = per_chip // blocks
    chunk = targets // steps
    sent = pl.ds(0, rows_sent)

    hap, mk = lax.axis_index("hap"), lax.axis_index("mk")
    chip, core = hap // CORES, hap % CORES
    partner = {"hap": chip * CORES + 1 - core, "mk": mk}

    def place(shift):
        return (mk + shift) % mk_count

    def peer(step, shift):
        return {"hap": ((chip + step) % chips) * CORES + 1 - core, "mk": place(shift)}

    allele_copy = pltpu.make_async_copy(allele_hbm, allele, small_sem.at[0])
    owner_copy = pltpu.make_async_copy(owner_hbm, owner, small_sem.at[1])
    allele_copy.start()
    owner_copy.start()
    post_copies = {}
    for g in range(GROUPS):
        first = g * local + (g > 0)
        taken = pl.ds(first, (g + 1) * local + 1 - first)
        for i in range(steps):
            rows = pl.ds(i * chunk, chunk)
            copy = pltpu.make_async_copy(
                post_hbm.at[taken, rows, :], post.at[taken, rows, :], post_sem.at[g, i]
            )
            copy.start()
            post_copies[g, i] = copy

    barrier = pltpu.get_barrier_semaphore()
    for step in range(chips):
        for shift in range(mk_count):
            pl.semaphore_signal(barrier, inc=1, device_id=peer(step, shift), device_id_type=MESH)

    order = sorted(range(1, chips), key=lambda s: abs(s - chips // 2 - 0.5)) + [0]

    allele_copy.wait()
    lane = lax.broadcasted_iota(jnp.int32, (block, LANES), 1) % half
    marker = lax.broadcasted_iota(jnp.int32, (block, LANES), 0)
    which, within = lane // pitch, lane % pitch
    allele_bf = allele[...].astype(F32).astype(BF16)
    row_lane = lax.broadcasted_iota(jnp.int32, (1, LANES), 1) % half
    row_which, row_within = row_lane // pitch, row_lane % pitch
    slots = []
    for g in range(GROUPS):
        wanted = (g * local + which // SIDES) * span + within
        spread = ((marker == wanted) & (within < span)).astype(F32).astype(BF16)
        wide = lax.dot_general(
            allele_bf, spread, (((0,), (0,)), ((), ())), preferred_element_type=F32
        )
        for k in range(g * local, (g + 1) * local + 1):
            inside = (g * local + row_which // SIDES + row_which % SIDES == k).astype(F32)
            ones = inside * (row_within == span).astype(F32)
            weights[len(slots)] = (wide * inside + ones).astype(BF16)
            slots.append((g, k))

    owner_copy.wait()
    owners = owner[...]
    table = (lax.broadcasted_iota(jnp.int32, (devices, targets), 0) == owners).astype(F32)
    before = (
        lax.broadcasted_iota(jnp.int32, (LANES, LANES), 0)
        < lax.broadcasted_iota(jnp.int32, (LANES, LANES), 1)
    ).astype(F32).astype(BF16)
    carry = jnp.zeros((devices, 1), F32)
    ranks = []
    for b in range(targets // LANES):
        piece = table[:, b * LANES : (b + 1) * LANES]
        count = jnp.dot(piece.astype(BF16), before, preferred_element_type=F32) + carry
        ranks.append(jnp.sum(piece * count, axis=0, keepdims=True))
        carry = carry + jnp.sum(piece, axis=1, keepdims=True)
    row_of = owners.astype(F32) * width + jnp.concatenate(ranks, axis=1)

    def fill_choose(step):
        for j in range(tiles_per_chip):
            first = (((chip + step) % chips) * tiles_per_chip + j) * LANES
            wanted = (lax.broadcasted_iota(jnp.int32, (LANES, targets), 0) + first).astype(F32)
            choose[step * tiles_per_chip + j] = (wanted == row_of).astype(F32).astype(BF16)

    def split(g, rows, total):
        high = total.astype(BF16)
        low = (total - high.astype(F32)).astype(BF16)
        left = lax.broadcasted_iota(jnp.int32, total.shape, 1) < half
        parts[g, rows, :] = jnp.where(left, high.astype(F32), low.astype(F32)).astype(BF16)

    def multiply(g, i):
        rows = pl.ds(i * chunk, chunk)
        post_copies[g, i].wait()
        total = held[rows, :] if g else jnp.zeros((chunk, LANES), F32)
        for k in range(g * local + (g > 0), (g + 1) * local + 1):
            mine_at = slots.index((g, k))
            if (g + 1, k) in slots:
                both = jnp.dot(
                    post[k, rows, :],
                    jnp.concatenate([weights[mine_at], weights[slots.index((g + 1, k))]], axis=1),
                    preferred_element_type=F32,
                )
                total = total + both[:, :LANES]
                held[rows, :] = both[:, LANES:]
            else:
                total = total + jnp.dot(post[k, rows, :], weights[mine_at], preferred_element_type=F32)
        split(g, rows, total)

    pair_copies = {}
    chip_copies = {}

    def send_pair(g, step):
        copies = []
        if step:
            copies.append((mine.at[g, step, core, :, sent, :], pair_in.at[g, step, :, sent, :], 0))
        else:
            for shift in range(mk_count):
                given = core if shift else 1 - core
                copies.append(
                    (
                        mine.at[g, step, given, place(shift), sent, :],
                        pair_in.at[g, step, place(shift), sent, :],
                        shift,
                    )
                )
        started = []
        for source, target, at in copies:
            copy = pltpu.make_async_remote_copy(
                src_ref=source,
                dst_ref=target,
                send_sem=pair_send.at[g, step, at],
                recv_sem=pair_recv.at[g, step, at],
                device_id=partner,
                device_id_type=MESH,
            )
            copy.start()
            started.append(copy)
        pair_copies[g, step] = started

    def permute(g, step):
        for j in range(tiles_per_chip):
            both = jnp.dot(
                choose[step * tiles_per_chip + j], parts[g], preferred_element_type=F32
            )
            turned = jnp.transpose(both)
            sums = turned[:half] + turned[half:]
            packed = block_transpose(
                [sums[q * pitch : (q + 1) * pitch] for q in range(blocks)], width
            )
            for e in range(blocks):
                index = j * blocks + e
                mine[g, step, index // mk_count, index % mk_count] = packed[e]
        send_pair(g, step)

    def pass_on(g, step):
        for copy in pair_copies[g, step]:
            copy.wait_recv()
        for shift in range(mk_count):
            at = place(shift)
            kept = 1 - core if step or shift else core
            reduced[g, step, at] = mine[g, step, kept, at] + pair_in[g, step, at]
            if step or shift:
                copy = pltpu.make_async_remote_copy(
                    src_ref=reduced.at[g, step, at, sent, :],
                    dst_ref=inbox.at[g, step, shift, sent, :],
                    send_sem=chip_send.at[g, step, shift],
                    recv_sem=chip_recv.at[g, step, shift],
                    device_id=peer(step, shift),
                    device_id_type=MESH,
                )
                copy.start()
                chip_copies[g, step, shift] = copy

    for i in range(steps):
        for step in order[i::steps]:
            fill_choose(step)
        multiply(0, i)
    pl.semaphore_wait(barrier, chips * mk_count)
    for step in order:
        permute(0, step)
    for i in range(steps):
        multiply(1, i)
    for step in order:
        pass_on(0, step)
    lag = 3
    for at, step in enumerate(order):
        permute(1, step)
        if at >= lag:
            pass_on(1, order[at - lag])
    for step in order[-lag:]:
        pass_on(1, step)

    rank = lax.broadcasted_iota(jnp.int32, (span, LANES), 0).astype(F32)
    right = (lax.broadcasted_iota(jnp.int32, (span, LANES), 1) // width % SIDES).astype(F32)
    weight = (rank + 0.5) / span
    weight = right * weight + (1.0 - right) * (1.0 - weight)
    for g in range(GROUPS):
        for shift in range(mk_count):
            total = None
            for step in reversed(order):
                if step or shift:
                    chip_copies[g, step, shift].wait_recv()
                    arrived = inbox[g, step, shift]
                else:
                    arrived = reduced[g, step, mk]
                total = arrived if total is None else total + arrived
            ratio = weight * (total[:span] / total[span : span + 1])
            source = (mk + mk_count - shift) % mk_count
            for l in range(local):
                at = source * block + (g * local + l) * span
                moved = ratio if l == 0 else pltpu.roll(ratio, LANES - l * SIDES * width, 1)
                stack[pl.ds(pl.multiple_of(at, span), span), :] = moved

    turned = jnp.transpose(stack[...])
    out_ref[...] = turned[:per_device] + turned[width : width + per_device]

    for g in range(GROUPS):
        for step in order:
            for copy in pair_copies[g, step]:
                copy.wait_send()
            for shift in range(mk_count):
                if step or shift:
                    chip_copies[g, step, shift].wait_send()


def solution(mesh):
    hap_count, mk_count = mesh.shape["hap"], mesh.shape["mk"]
    steps = 4

    def on_device(posterior, alleles, owner_map):
        anchors, targets, refs = posterior.shape
        block = alleles.shape[1]
        intervals = anchors - 1
        span = block // intervals
        chips = hap_count // CORES
        per_device = targets // (hap_count * mk_count)
        width = LANES // (intervals // GROUPS * SIDES)
        positions = width * hap_count * mk_count
        exchange = (GROUPS, chips, mk_count, 2 * span, LANES)
        scratch = [
            pltpu.VMEM(posterior.shape, BF16),
            pltpu.VMEM((block, refs), jnp.int32),
            pltpu.VMEM((1, targets), jnp.int32),
            pltpu.VMEM((anchors + GROUPS - 1, refs, LANES), BF16),
            pltpu.VMEM((positions // LANES, LANES, targets), BF16),
            pltpu.VMEM((targets, LANES), F32),
            pltpu.VMEM((GROUPS, targets, LANES), BF16),
            pltpu.VMEM((GROUPS, chips, CORES, mk_count, 2 * span, LANES), F32),
            pltpu.VMEM(exchange, F32),
            pltpu.VMEM(exchange, F32),
            pltpu.VMEM(exchange, F32),
            pltpu.VMEM((mk_count * block, LANES), F32),
            pltpu.SemaphoreType.DMA((GROUPS, steps)),
            pltpu.SemaphoreType.DMA((2,)),
        ] + [pltpu.SemaphoreType.DMA((GROUPS, chips, mk_count))] * 4
        return pl.pallas_call(
            functools.partial(kernel, hap_count, mk_count, steps),
            out_shape=jax.ShapeDtypeStruct((per_device, mk_count * block), F32),
            in_specs=[pl.BlockSpec(memory_space=pltpu.HBM)] * 3,
            out_specs=pl.BlockSpec(memory_space=pltpu.VMEM),
            scratch_shapes=scratch,
            compiler_params=pltpu.CompilerParams(
                collective_id=0, has_side_effects=True, vmem_limit_bytes=63 * 1024 * 1024
            ),
        )(posterior, alleles.T, owner_map.reshape(1, targets))

    placed = (P("mk", None, "hap"), P("hap", "mk"), P())
    return jax.shard_map(
        on_device, mesh=mesh, in_specs=placed, out_specs=P(("hap", "mk"), None), check_vma=False
    )
```

time: 22.6 us -> 27.8 us (1.23)
  Pallas kernels: 20.3 us -> 26.2 us
  local copies, waits for them, and re-layouts: 2.2 us -> 1.32 us
    pallas_call x1, Pallas kernels: 20.3 us -> 26.2 us  [on_device(): pl.pallas_call(functools.partial(kernel, hap_count, mk_count, steps), out...]
    unnamed x5 -> x1, local copies, waits for them, and re-layouts: 2.2 us -> 1.32 us
where the time goes in v1:
time: 27.8 us; the launch traced here: 27.5 us
  Pallas kernels  26.2 us (94%)
  local copies, waits for them, and re-layouts  1.32 us (5%)
    pallas_call x1, Pallas kernels, on_device(): pl.pallas_call(functools.partial(kernel, hap_count, mk_count, steps), out...  26.2 us
    unnamed x1, local copies, waits for them, and re-layouts  1.32 us

profile of v1, /device:TPU:0, one launch (start us, length us, event | category | flops | bytes accessed | tf_op | source)
XLA Modules:
  0.0 27.5 jit_solution(15681213635523115507)
XLA Ops:
  0.0 26.2 %shard_map.37 = f32[32,64]{1,0:T(8,128)} custom-call(bf16[5,1024,1024]{2,1,0:T(8,128)(2,1)} %post_hbm.1, s32[32,1024]{1,0:T(8,128)} %bitcast.2, s32[1,1024]{1,0:T(1,128)} %bitcast.3), custom_call_target="tpu_custom_call" | custom-call | tf_op jit(solution)/shard_map/pallas_call | solution.py:327
  26.2 1.3 %copy.5 = f32[32,64]{1,0:T(8,128)} copy(f32[32,64]{1,0:T(8,128)} %shard_map.37) | data formatting | bytes 16384

commit v2 on v1

v2 whole, which is shorter than its diff:
```python
import functools

import jax
import jax.numpy as jnp
from jax import lax
from jax.experimental import pallas as pl
from jax.experimental.pallas import tpu as pltpu
from jax.sharding import PartitionSpec as P

LANES = 128
CORES = 2
GROUPS = 2
SIDES = 2
MESH = pl.DeviceIdType.MESH
F32 = jnp.float32
BF16 = jnp.bfloat16


def block_transpose(tiles, width):
    lane = lax.broadcasted_iota(jnp.int32, tiles[0].shape, 1) // width
    count = len(tiles)
    bit = 1
    while bit < count:
        swapped = list(tiles)
        low = lane // bit % 2 == 0
        for i in range(count):
            if i & bit == 0:
                a, b = tiles[i], tiles[i + bit]
                swapped[i] = jnp.where(low, a, pltpu.roll(b, bit * width, 1))
                swapped[i + bit] = jnp.where(low, pltpu.roll(a, LANES - bit * width, 1), b)
        tiles = swapped
        bit *= 2
    return tiles


def kernel(
    hap_count,
    mk_count,
    steps,
    post_hbm,
    allele_hbm,
    owner_hbm,
    out_ref,
    post,
    allele,
    owner,
    wide,
    weights,
    choose,
    held,
    parts,
    mine,
    pair_in,
    reduced,
    inbox,
    stack,
    post_sem,
    small_sem,
    pair_send,
    pair_recv,
    chip_send,
    chip_recv,
):
    anchors, targets, refs = post.shape
    block = allele.shape[0]
    intervals = anchors - 1
    span = block // intervals
    local = intervals // GROUPS
    blocks = local * SIDES
    width = LANES // blocks
    pitch = 2 * span
    half = blocks * pitch
    chips = hap_count // CORES
    devices = hap_count * mk_count
    per_device = targets // devices
    per_chip = CORES * mk_count
    tiles_per_chip = per_chip // blocks
    chunk = targets // steps
    sent = pl.ds(0, span + 1)
    far = chips * mk_count - 1

    hap, mk = lax.axis_index("hap"), lax.axis_index("mk")
    chip, core = hap // CORES, hap % CORES
    partner = {"hap": chip * CORES + 1 - core, "mk": mk}

    def place(shift):
        return (mk + shift) % mk_count

    def slot(step, shift):
        return (step - 1) % chips * mk_count + mk_count - 1 - shift

    def peer(step, shift):
        return {"hap": ((chip + step) % chips) * CORES + 1 - core, "mk": place(shift)}

    def groups_of(k):
        return [g for g in range(GROUPS) if g * local <= k <= (g + 1) * local]

    allele_copy = pltpu.make_async_copy(allele_hbm, allele, small_sem.at[0])
    owner_copy = pltpu.make_async_copy(owner_hbm, owner, small_sem.at[1])
    allele_copy.start()
    owner_copy.start()
    post_copies = {}
    for k in range(anchors):
        for i in range(steps):
            rows = pl.ds(i * chunk, chunk)
            post_copies[k, i] = pltpu.make_async_copy(
                post_hbm.at[k, rows, :], post.at[k, rows, :], post_sem.at[k, i]
            )
    for i in range(steps):
        post_copies[0, i].start()

    barrier = pltpu.get_barrier_semaphore()
    for step in range(chips):
        for shift in range(mk_count):
            pl.semaphore_signal(barrier, inc=1, device_id=peer(step, shift), device_id_type=MESH)

    order = list(range(1, chips)) + [0]

    lane = lax.broadcasted_iota(jnp.int32, (block, GROUPS * LANES), 1)
    marker = lax.broadcasted_iota(jnp.int32, (block, GROUPS * LANES), 0)
    which, within = lane % half // pitch, lane % pitch
    wanted = (lane // LANES * local + which // SIDES) * span + within
    spread = ((marker == wanted) & (within < span)).astype(F32).astype(BF16)
    with jax.named_scope("allele_wait"):
        allele_copy.wait()
        for at, copy in post_copies.items():
            if at[0]:
                copy.start()
    wide[...] = lax.dot_general(
        allele[...].astype(F32).astype(BF16),
        spread,
        (((0,), (0,)), ((), ())),
        preferred_element_type=F32,
    ).astype(BF16)

    def columns(k):
        groups = groups_of(k)
        return pl.ds(groups[0] * LANES, len(groups) * LANES)

    def fill_weights(k):
        groups = groups_of(k)
        lanes = lax.broadcasted_iota(jnp.int32, (1, len(groups) * LANES), 1) + groups[0] * LANES
        at = lanes % half // pitch
        inside = (lanes // LANES * local + at // SIDES + at % SIDES == k).astype(F32)
        ones = (inside * (lanes % pitch == span).astype(F32)).astype(BF16)
        weights[k, :, columns(k)] = wide[:, columns(k)] * inside.astype(BF16) + ones

    def fill_choose(batch, row_of):
        for step in batch:
            for j in range(tiles_per_chip):
                first = (((chip + step) % chips) * tiles_per_chip + j) * LANES
                wanted = (lax.broadcasted_iota(jnp.int32, (LANES, targets), 0) + first).astype(F32)
                choose[pl.ds((step * tiles_per_chip + j) * LANES, LANES), :] = (wanted == row_of).astype(F32).astype(BF16)

    def wait_post(k, i):
        with jax.named_scope(f"wait{k}{i}"):
            post_copies[k, i].wait()

    def multiply(k, i):
        piece = chunk // 2
        halves = [pl.ds(i * chunk + n * piece, piece) for n in range(2)]
        outs = [
            jnp.dot(post[k, rows, :], weights[k, :, columns(k)], preferred_element_type=F32)
            for rows in halves
        ]
        for rows, out in zip(halves, outs):
            for n, g in enumerate(groups_of(k)):
                total = out[:, n * LANES : (n + 1) * LANES]
                if k > g * local:
                    total = total + held[g, rows, :]
                if k < (g + 1) * local:
                    held[g, rows, :] = total
                else:
                    high = total.astype(BF16)
                    low = (total - high.astype(F32)).astype(BF16)
                    left = lax.broadcasted_iota(jnp.int32, total.shape, 1) < half
                    both = jnp.where(left, high.astype(F32), low.astype(F32))
                    parts[g, rows, :] = both.astype(BF16)

    def pair_copy(source, target, g):
        return pltpu.make_async_remote_copy(
            src_ref=source,
            dst_ref=target,
            send_sem=pair_send.at[g],
            recv_sem=pair_recv.at[g],
            device_id=partner,
            device_id_type=MESH,
        )

    def chip_copy(source, target, g, device):
        return pltpu.make_async_remote_copy(
            src_ref=source,
            dst_ref=target,
            send_sem=chip_send.at[g],
            recv_sem=chip_recv.at[g],
            device_id=device,
            device_id_type=MESH,
        )

    def send_pair(g):
        for step in order:
            if step:
                pair_copy(
                    mine.at[g, step, core, :, sent, :], pair_in.at[g, step, :, sent, :], g
                ).start()
                continue
            for shift in range(mk_count):
                given = core if shift else 1 - core
                at = place(shift)
                pair_copy(
                    mine.at[g, step, given, at, sent, :], pair_in.at[g, step, at, sent, :], g
                ).start()

    def whole_pair(g):
        return pair_copy(mine.at[g, :, core, :, sent, :], pair_in.at[g, :, :, sent, :], g)

    def whole_chip(g):
        taken = pl.ds(0, far)
        return chip_copy(
            reduced.at[g, taken, sent, :], inbox.at[g, taken, sent, :], g, peer(1, 0)
        )

    def permute(g):
        tiles = [(step, j) for step in range(chips) for j in range(tiles_per_chip)]
        batch = min(4, len(tiles))
        for first in range(0, len(tiles), batch):
            out = jnp.dot(
                choose[first * LANES : (first + batch) * LANES, :],
                parts[g],
                preferred_element_type=F32,
            )
            for n, (step, j) in enumerate(tiles[first : first + batch]):
                turned = jnp.transpose(out[n * LANES : (n + 1) * LANES])
                sums = turned[:half] + turned[half:]
                packed = block_transpose(
                    [sums[q * pitch : (q + 1) * pitch] for q in range(blocks)], width
                )
                for e in range(blocks):
                    index = j * blocks + e
                    mine[g, step, index // mk_count, index % mk_count] = packed[e]

    def pass_on(g):
        whole_pair(g).wait_recv()
        for step in order:
            for shift in reversed(range(mk_count)):
                at = place(shift)
                kept = 1 - core if step or shift else core
                to = slot(step, shift)
                reduced[g, to] = mine[g, step, kept, at] + pair_in[g, step, at]
                if step or shift:
                    chip_copy(
                        reduced.at[g, to, sent, :], inbox.at[g, to, sent, :], g, peer(step, shift)
                    ).start()

    fill_weights(0)
    with jax.named_scope("owner_wait"):
        owner_copy.wait()
    wait_post(0, 0)
    with jax.named_scope("multiply0"):
        multiply(0, 0)
        owners = owner[...]
        table = (lax.broadcasted_iota(jnp.int32, (devices, targets), 0) == owners).astype(F32)
        before = (
            lax.broadcasted_iota(jnp.int32, (LANES, LANES), 0)
            < lax.broadcasted_iota(jnp.int32, (LANES, LANES), 1)
        ).astype(F32).astype(BF16)
        carry = jnp.zeros((devices, 1), F32)
        ranks = []
        for b in range(targets // LANES):
            piece = table[:, b * LANES : (b + 1) * LANES]
            count = jnp.dot(piece.astype(BF16), before, preferred_element_type=F32) + carry
            ranks.append(jnp.sum(piece * count, axis=0, keepdims=True))
            carry = carry + jnp.sum(piece, axis=1, keepdims=True)
        row_of = owners.astype(F32) * width + jnp.concatenate(ranks, axis=1)
        fill_weights(1)
        for i in range(1, steps):
            wait_post(0, i)
            multiply(0, i)
        fill_weights(2)
    early = local * steps
    done = 0
    for k in range(1, local + 1):
        with jax.named_scope(f"multiply{k}"):
            for i in range(steps):
                wait_post(k, i)
            for i in range(steps):
                fill_choose(order[done::early], row_of)
                done += 1
                multiply(k, i)
            if k + 2 < anchors:
                fill_weights(k + 2)
    tail = [(k, i) for k in range(local + 1, anchors) for i in range(steps)]
    wait_post(*tail[0])
    with jax.named_scope("permuteA"):
        permute(0)
        multiply(*tail[0])
    with jax.named_scope("barrier"):
        pl.semaphore_wait(barrier, far + 1)
    with jax.named_scope("sendA"):
        send_pair(0)
    with jax.named_scope("multiplyB"):
        for k, i in tail[1:]:
            wait_post(k, i)
        for k, i in tail[1:]:
            multiply(k, i)
    with jax.named_scope("passA"):
        pass_on(0)
    with jax.named_scope("permuteB"):
        permute(1)
    with jax.named_scope("sendB"):
        send_pair(1)
    with jax.named_scope("passB"):
        pass_on(1)

    rank = lax.broadcasted_iota(jnp.int32, (span, LANES), 0).astype(F32)
    right = (lax.broadcasted_iota(jnp.int32, (span, LANES), 1) // width % SIDES).astype(F32)
    weight = (rank + 0.5) / span
    weight = right * weight + (1.0 - right) * (1.0 - weight)
    for g in range(GROUPS):
        with jax.named_scope(f"gather{g}"):
            whole_chip(g).wait_recv()
        for shift in range(mk_count):
            total = None
            for step in reversed(order):
                at = slot(step, shift)
                arrived = inbox[g, at] if step or shift else reduced[g, at]
                total = arrived if total is None else total + arrived
            ratio = weight * (total[:span] / total[span : span + 1])
            source = (mk + mk_count - shift) % mk_count
            for l in range(local):
                at = source * block + (g * local + l) * span
                moved = ratio if l == 0 else pltpu.roll(ratio, LANES - l * SIDES * width, 1)
                stack[pl.ds(pl.multiple_of(at, span), span), :] = moved
    with jax.named_scope("finish"):
        turned = jnp.transpose(stack[...])
        out_ref[...] = turned[:per_device] + turned[width : width + per_device]
    with jax.named_scope("drain"):
        for g in range(GROUPS):
            whole_pair(g).wait_send()
            whole_chip(g).wait_send()


def solution(mesh):
    hap_count, mk_count = mesh.shape["hap"], mesh.shape["mk"]
    steps = 2

    def on_device(posterior, alleles, owner_map):
        anchors, targets, refs = posterior.shape
        block = alleles.shape[1]
        intervals = anchors - 1
        span = block // intervals
        chips = hap_count // CORES
        per_device = targets // (hap_count * mk_count)
        width = LANES // (intervals // GROUPS * SIDES)
        positions = width * hap_count * mk_count
        slots = (GROUPS, chips * mk_count, 2 * span, LANES)
        scratch = [
            pltpu.VMEM(posterior.shape, BF16),
            pltpu.VMEM((block, refs), jnp.int32),
            pltpu.VMEM((1, targets), jnp.int32),
            pltpu.VMEM((refs, GROUPS * LANES), BF16),
            pltpu.VMEM((anchors, refs, GROUPS * LANES), BF16),
            pltpu.VMEM((positions, targets), BF16),
            pltpu.VMEM((GROUPS, targets, LANES), F32),
            pltpu.VMEM((GROUPS, targets, LANES), BF16),
            pltpu.VMEM((GROUPS, chips, CORES, mk_count, 2 * span, LANES), F32),
            pltpu.VMEM((GROUPS, chips, mk_count, 2 * span, LANES), F32),
            pltpu.VMEM(slots, F32),
            pltpu.VMEM(slots, F32),
            pltpu.VMEM((mk_count * block, LANES), F32),
            pltpu.SemaphoreType.DMA((anchors, steps)),
            pltpu.SemaphoreType.DMA((2,)),
        ] + [pltpu.SemaphoreType.DMA((GROUPS,))] * 4
        return pl.pallas_call(
            functools.partial(kernel, hap_count, mk_count, steps),
            out_shape=pltpu.VMEM((per_device, mk_count * block), F32),
            in_specs=[pl.BlockSpec(memory_space=pltpu.HBM)] * 3,
            out_specs=pl.BlockSpec(memory_space=pltpu.VMEM),
            scratch_shapes=scratch,
            compiler_params=pltpu.CompilerParams(
                collective_id=0, has_side_effects=True, vmem_limit_bytes=60000000
            ),
        )(posterior, alleles.T, owner_map.reshape(1, targets))

    placed = (P("mk", None, "hap"), P("hap", "mk"), P())
    return jax.shard_map(
        on_device, mesh=mesh, in_specs=placed, out_specs=P(("hap", "mk"), None), check_vma=False
    )
```

time: 27.8 us -> 17.7 us (0.64)
  Pallas kernels: 26.2 us -> 16.9 us
  local copies, waits for them, and re-layouts: 1.32 us -> 0.61 us
    pallas_call x1, Pallas kernels: 26.2 us -> 16.9 us  [on_device(): pl.pallas_call(functools.partial(kernel, hap_count, mk_count, steps), out...]
    unnamed x1, local copies, waits for them, and re-layouts: 1.32 us -> 0.61 us
where the time goes in v2:
time: 17.7 us; the launch traced here: 17.5 us
  Pallas kernels  16.9 us (95%)
  local copies, waits for them, and re-layouts  0.61 us (3%)
    pallas_call x1, Pallas kernels, on_device(): pl.pallas_call(functools.partial(kernel, hap_count, mk_count, steps), out...  16.9 us
    unnamed x1, local copies, waits for them, and re-layouts  0.61 us

profile of v2, /device:TPU:0, one launch (start us, length us, event | category | flops | bytes accessed | tf_op | source)
XLA Modules:
  0.0 17.5 jit_solution(6474207290786326373)
XLA Ops:
  0.0 16.9 %shard_map.37 = f32[32,64]{1,0:T(8,128)S(1)} custom-call(bf16[5,1024,1024]{2,1,0:T(8,128)(2,1)} %post_hbm.1, s32[32,1024]{1,0:T(8,128)} %bitcast.2, s32[1,1024]{1,0:T(1,128)} %bitcast.3), custom_call_target="tpu_custom_call" | custom-call | tf_op jit(solution)/shard_map/pallas_call | solution.py:374
  16.9 0.6 %copy.5 = f32[32,64]{1,0:T(8,128)} copy(f32[32,64]{1,0:T(8,128)S(1)} %shard_map.37) | data formatting | bytes 16384

commit v3 on v2

v3 whole, which is shorter than its diff:
```python
import functools

import jax
import jax.numpy as jnp
from jax import lax
from jax.experimental import pallas as pl
from jax.experimental.pallas import tpu as pltpu
from jax.sharding import PartitionSpec as P

LANES = 128
CORES = 2
GROUPS = 2
SIDES = 2
MESH = pl.DeviceIdType.MESH
F32 = jnp.float32
BF16 = jnp.bfloat16


def block_transpose(tiles, width):
    lane = lax.broadcasted_iota(jnp.int32, tiles[0].shape, 1) // width
    count = len(tiles)
    bit = 1
    while bit < count:
        swapped = list(tiles)
        low = lane // bit % 2 == 0
        for i in range(count):
            if i & bit == 0:
                a, b = tiles[i], tiles[i + bit]
                swapped[i] = jnp.where(low, a, pltpu.roll(b, bit * width, 1))
                swapped[i + bit] = jnp.where(low, pltpu.roll(a, LANES - bit * width, 1), b)
        tiles = swapped
        bit *= 2
    return tiles


def kernel(
    hap_count,
    mk_count,
    post_hbm,
    allele_hbm,
    owner_hbm,
    out_ref,
    post,
    allele,
    owner,
    wide,
    weights,
    held,
    parts,
    mine,
    pair_in,
    reduced,
    inbox,
    stack,
    post_sem,
    small_sem,
    pair_send,
    pair_recv,
    chip_send,
    chip_recv,
):
    anchors, targets, refs = post.shape
    block = allele.shape[0]
    intervals = anchors - 1
    span = block // intervals
    local = intervals // GROUPS
    blocks = local * SIDES
    width = LANES // blocks
    values = GROUPS * span
    chips = hap_count // CORES
    devices = hap_count * mk_count
    per_device = targets // devices
    tiles_per_chip = CORES * mk_count // blocks
    sent = pl.ds(0, span + 1)
    far = chips * mk_count - 1

    hap, mk = lax.axis_index("hap"), lax.axis_index("mk")
    chip, core = hap // CORES, hap % CORES
    partner = {"hap": chip * CORES + 1 - core, "mk": mk}

    def place(shift):
        return (mk + shift) % mk_count

    def slot(step, shift):
        return (step - 1) % chips * mk_count + mk_count - 1 - shift

    def peer(step, shift):
        return {"hap": ((chip + step) % chips) * CORES + 1 - core, "mk": place(shift)}

    allele_copy = pltpu.make_async_copy(allele_hbm, allele, small_sem.at[0])
    owner_copy = pltpu.make_async_copy(owner_hbm, owner, small_sem.at[1])
    allele_copy.start()
    owner_copy.start()
    post_copies = [
        pltpu.make_async_copy(post_hbm.at[k], post.at[k], post_sem.at[k]) for k in range(anchors)
    ]
    for copy in post_copies:
        copy.start(priority=1)

    barrier = pltpu.get_barrier_semaphore()
    for step in range(chips):
        for shift in range(mk_count):
            pl.semaphore_signal(barrier, inc=1, device_id=peer(step, shift), device_id_type=MESH)

    def parts_of(lane):
        at, within = lane // width, lane % width
        is_value = within < values
        group = within // span % GROUPS
        interval = group * local + at // SIDES
        used = is_value | (within % span == 0)
        return interval, interval + at % SIDES, within % span, is_value, used

    lane = lax.broadcasted_iota(jnp.int32, (block, LANES), 1)
    marker = lax.broadcasted_iota(jnp.int32, (block, LANES), 0)
    interval, _, rank, is_value, _ = parts_of(lane)
    spread = ((marker == interval * span + rank) & is_value).astype(F32).astype(BF16)
    with jax.named_scope("allele_wait"):
        allele_copy.wait()
    wide[...] = lax.dot_general(
        allele[...].astype(F32).astype(BF16),
        spread,
        (((0,), (0,)), ((), ())),
        preferred_element_type=F32,
    ).astype(BF16)

    _, anchor, _, row_value, row_used = parts_of(lax.broadcasted_iota(jnp.int32, (1, LANES), 1))

    def fill_weights(k):
        inside = ((anchor == k) & row_used).astype(F32)
        ones = inside * (1.0 - row_value.astype(F32))
        weights[k] = wide[...] * inside.astype(BF16) + ones.astype(BF16)

    def multiply(k):
        half = targets // 2
        high_lanes, low_lanes = pl.ds(0, LANES), pl.ds(LANES, LANES)
        for n in range(2):
            rows = pl.ds(n * half, half)
            total = jnp.dot(post[k, rows, :], weights[k], preferred_element_type=F32)
            if k % (local + 1):
                total = total + held[rows, :]
            if k == anchors - 1:
                total = total + parts[rows, low_lanes].astype(F32)
                total = total + parts[rows, high_lanes].astype(F32)
            if k in (local, anchors - 1):
                high = total.astype(BF16)
                parts[rows, high_lanes] = high
                parts[rows, low_lanes] = (total - high.astype(F32)).astype(BF16)
            else:
                held[rows, :] = total

    def pair_copy(source, target, g):
        return pltpu.make_async_remote_copy(
            src_ref=source,
            dst_ref=target,
            send_sem=pair_send.at[g],
            recv_sem=pair_recv.at[g],
            device_id=partner,
            device_id_type=MESH,
        )

    def chip_copy(source, target, g, device):
        return pltpu.make_async_remote_copy(
            src_ref=source,
            dst_ref=target,
            send_sem=chip_send.at[g],
            recv_sem=chip_recv.at[g],
            device_id=device,
            device_id_type=MESH,
        )

    def send_pair(g):
        for step in every:
            if step:
                pair_copy(
                    mine.at[g, step, core, :, sent, :], pair_in.at[g, step, :, sent, :], g
                ).start()
                continue
            for shift in range(mk_count):
                given = core if shift else 1 - core
                at = place(shift)
                pair_copy(
                    mine.at[g, step, given, at, sent, :], pair_in.at[g, step, at, sent, :], g
                ).start()

    def whole_pair(g):
        return pair_copy(mine.at[g, :, core, :, sent, :], pair_in.at[g, :, :, sent, :], g)

    def whole_chip(g):
        taken = pl.ds(0, far)
        return chip_copy(
            reduced.at[g, taken, sent, :], inbox.at[g, taken, sent, :], g, peer(1, 0)
        )

    def permute(g):
        tiles = [(step, j) for step in every for j in range(tiles_per_chip)]
        batch = 4
        for at in range(0, len(tiles), batch):
            now = tiles[at : at + batch]
            chosen = []
            for step, j in now:
                first = (((chip + step) % chips) * tiles_per_chip + j) * LANES
                wanted = (lax.broadcasted_iota(jnp.int32, (LANES, targets), 0) + first).astype(F32)
                chosen.append((wanted == row_of).astype(F32).astype(BF16))
            out = jnp.dot(
                jnp.concatenate(chosen, axis=0), parts[...], preferred_element_type=F32
            )
            out = out[:, :LANES] + out[:, LANES:]
            for n, (step, j) in enumerate(now):
                turned = jnp.transpose(out[n * LANES : (n + 1) * LANES])
                tall = []
                for q in range(blocks):
                    top = q * width + g * span
                    bottom = top + values
                    tall.append(
                        jnp.concatenate([turned[top : top + span], turned[bottom : bottom + span]])
                    )
                packed = block_transpose(tall, width)
                for e in range(blocks):
                    index = j * blocks + e
                    mine[g, step, index // mk_count, index % mk_count] = packed[e]

    def pass_on(g):
        whole_pair(g).wait_recv()
        for step in every[1:] + every[:1]:
            for shift in reversed(range(mk_count)):
                at = place(shift)
                kept = 1 - core if step or shift else core
                to = slot(step, shift)
                reduced[g, to] = mine[g, step, kept, at] + pair_in[g, step, at]
                if step or shift:
                    chip_copy(
                        reduced.at[g, to, sent, :], inbox.at[g, to, sent, :], g, peer(step, shift)
                    ).start()

    fill_weights(0)
    with jax.named_scope("owner_wait"):
        owner_copy.wait()
    owners = owner[...]
    table = (lax.broadcasted_iota(jnp.int32, (devices, targets), 0) == owners).astype(F32)
    before = (
        lax.broadcasted_iota(jnp.int32, (LANES, LANES), 0)
        < lax.broadcasted_iota(jnp.int32, (LANES, LANES), 1)
    ).astype(F32).astype(BF16)
    carry = jnp.zeros((devices, 1), F32)
    ranks = []
    for b in range(targets // LANES):
        piece = table[:, b * LANES : (b + 1) * LANES]
        count = jnp.dot(piece.astype(BF16), before, preferred_element_type=F32) + carry
        ranks.append(jnp.sum(piece * count, axis=0, keepdims=True))
        carry = carry + jnp.sum(piece, axis=1, keepdims=True)
    row_of = owners.astype(F32) * width + jnp.concatenate(ranks, axis=1)

    every = list(range(chips))
    for k in range(anchors):
        with jax.named_scope(f"wait{k}"):
            post_copies[k].wait()
        with jax.named_scope(f"multiply{k}"):
            if k == local + 1:
                permute(0)
            multiply(k)
            if k + 1 < anchors:
                fill_weights(k + 1)
            if k == anchors - 1:
                permute(1)
        if k == local + 1:
            with jax.named_scope("barrier"):
                pl.semaphore_wait(barrier, far + 1)
            with jax.named_scope("sendA"):
                send_pair(0)
    with jax.named_scope("sendB"):
        send_pair(1)
    with jax.named_scope("passA"):
        pass_on(0)
    with jax.named_scope("passB"):
        pass_on(1)

    rank = lax.broadcasted_iota(jnp.int32, (span, LANES), 0).astype(F32)
    right = (lax.broadcasted_iota(jnp.int32, (span, LANES), 1) // width % SIDES).astype(F32)
    weight = (rank + 0.5) / span
    weight = right * weight + (1.0 - right) * (1.0 - weight)
    for g in range(GROUPS):
        with jax.named_scope(f"gather{g}"):
            whole_chip(g).wait_recv()
        for shift in range(mk_count):
            total = None
            for step in every:
                at = slot(step, shift)
                arrived = inbox[g, at] if step or shift else reduced[g, at]
                total = arrived if total is None else total + arrived
            ratio = weight * (total[:span] / total[span : span + 1])
            source = (mk + mk_count - shift) % mk_count
            for l in range(local):
                at = source * block + (g * local + l) * span
                moved = ratio if l == 0 else pltpu.roll(ratio, LANES - l * SIDES * width, 1)
                stack[pl.ds(pl.multiple_of(at, span), span), :] = moved
    with jax.named_scope("finish"):
        turned = jnp.transpose(stack[...])
        out_ref[...] = turned[:per_device] + turned[width : width + per_device]
    with jax.named_scope("drain"):
        for g in range(GROUPS):
            whole_pair(g).wait_send()
            whole_chip(g).wait_send()


def solution(mesh):
    hap_count, mk_count = mesh.shape["hap"], mesh.shape["mk"]

    def on_device(posterior, alleles, owner_map):
        anchors, targets, refs = posterior.shape
        block = alleles.shape[1]
        intervals = anchors - 1
        span = block // intervals
        chips = hap_count // CORES
        per_device = targets // (hap_count * mk_count)
        slots = (GROUPS, chips * mk_count, 2 * span, LANES)
        scratch = [
            pltpu.VMEM(posterior.shape, BF16),
            pltpu.VMEM((block, refs), jnp.int32),
            pltpu.VMEM((1, targets), jnp.int32),
            pltpu.VMEM((refs, LANES), BF16),
            pltpu.VMEM((anchors, refs, LANES), BF16),
            pltpu.VMEM((targets, LANES), F32),
            pltpu.VMEM((targets, 2 * LANES), BF16),
            pltpu.VMEM((GROUPS, chips, CORES, mk_count, 2 * span, LANES), F32),
            pltpu.VMEM((GROUPS, chips, mk_count, 2 * span, LANES), F32),
            pltpu.VMEM(slots, F32),
            pltpu.VMEM(slots, F32),
            pltpu.VMEM((mk_count * block, LANES), F32),
            pltpu.SemaphoreType.DMA((anchors,)),
            pltpu.SemaphoreType.DMA((2,)),
        ] + [pltpu.SemaphoreType.DMA((GROUPS,))] * 4
        return pl.pallas_call(
            functools.partial(kernel, hap_count, mk_count),
            out_shape=pltpu.VMEM((per_device, mk_count * block), F32),
            in_specs=[pl.BlockSpec(memory_space=pltpu.HBM)] * 3,
            out_specs=pl.BlockSpec(memory_space=pltpu.VMEM),
            scratch_shapes=scratch,
            compiler_params=pltpu.CompilerParams(
                collective_id=0, has_side_effects=True, vmem_limit_bytes=60000000
            ),
        )(posterior, alleles.T, owner_map.reshape(1, targets))

    placed = (P("mk", None, "hap"), P("hap", "mk"), P())
    return jax.shard_map(
        on_device, mesh=mesh, in_specs=placed, out_specs=P(("hap", "mk"), None), check_vma=False
    )
```

time: 17.7 us -> 17 us (0.960)
  Pallas kernels: 16.9 us -> 16.2 us
    pallas_call x1, Pallas kernels: 16.9 us -> 16.2 us  [on_device(): pl.pallas_call(functools.partial(kernel, hap_count, mk_count), out_shape=...]
where the time goes in v3:
time: 17 us; the launch traced here: 16.8 us
  Pallas kernels  16.2 us (95%)
  local copies, waits for them, and re-layouts  0.61 us (4%)
    pallas_call x1, Pallas kernels, on_device(): pl.pallas_call(functools.partial(kernel, hap_count, mk_count), out_shape=...  16.2 us
    unnamed x1, local copies, waits for them, and re-layouts  0.61 us

profile of v3, /device:TPU:0, one launch (start us, length us, event | category | flops | bytes accessed | tf_op | source)
XLA Modules:
  0.0 16.8 jit_solution(8933104023088679749)
XLA Ops:
  0.0 16.2 %shard_map.37 = f32[32,64]{1,0:T(8,128)S(1)} custom-call(bf16[5,1024,1024]{2,1,0:T(8,128)(2,1)} %post_hbm.1, s32[32,1024]{1,0:T(8,128)} %bitcast.2, s32[1,1024]{1,0:T(1,128)} %bitcast.3), custom_call_target="tpu_custom_call" | custom-call | tf_op jit(solution)/shard_map/pallas_call | solution.py:332
  16.2 0.6 %copy.5 = f32[32,64]{1,0:T(8,128)} copy(f32[32,64]{1,0:T(8,128)S(1)} %shard_map.37) | data formatting | bytes 16384

commit v4 on v3

--- a/solution.py
+++ b/solution.py
@@ -193,7 +193,7 @@
 
     def permute(g):
         tiles = [(step, j) for step in every for j in range(tiles_per_chip)]
-        batch = 4
+        batch = 2
         for at in range(0, len(tiles), batch):
             now = tiles[at : at + batch]
             chosen = []

time: 17 us -> 16.9 us (level)
  no operation moved by 1% of the time
where the time goes in v4:
time: 16.9 us; the launch traced here: 16.8 us
  Pallas kernels  16.2 us (96%)
  local copies, waits for them, and re-layouts  0.61 us (4%)
    pallas_call x1, Pallas kernels, on_device(): pl.pallas_call(functools.partial(kernel, hap_count, mk_count), out_shape=...  16.2 us
    unnamed x1, local copies, waits for them, and re-layouts  0.61 us

profile of v4, /device:TPU:0, one launch (start us, length us, event | category | flops | bytes accessed | tf_op | source)
XLA Modules:
  0.0 16.8 jit_solution(16095334701833758095)
XLA Ops:
  0.0 16.2 %shard_map.37 = f32[32,64]{1,0:T(8,128)S(1)} custom-call(bf16[5,1024,1024]{2,1,0:T(8,128)(2,1)} %post_hbm.1, s32[32,1024]{1,0:T(8,128)} %bitcast.2, s32[1,1024]{1,0:T(1,128)} %bitcast.3), custom_call_target="tpu_custom_call" | custom-call | tf_op jit(solution)/shard_map/pallas_call | solution.py:332
  16.2 0.6 %copy.5 = f32[32,64]{1,0:T(8,128)} copy(f32[32,64]{1,0:T(8,128)S(1)} %shard_map.37) | data formatting | bytes 16384
